TPU v7x, 32 devices: a whole 2x2x4 slice. The times are simulated.
32 devices in a mesh: blk: 16 (over z, x, core), own: 2 (over y).
Axes of the slice: x: 2, y: 2, z: 4, core: 2. Of those that a mesh axis runs over, the one named last changes fastest.
Arguments:
- embeddings: bfloat16 [4096, 768], P(('blk', 'own')), may hold values from -320 to 320
- centroids: bfloat16 [16384, 768], P('blk'), may hold values from -4 to 4
- log_weight: float32 [16384], P('blk'), may hold values from -0.5 to 1.6
Outputs:
- new_centroids: float32 [16384, 768], P(('blk', 'own'))
- counts: float32 [16384], P(('blk', 'own'))
- log_norm: float32 [4096], P(('blk', 'own'))
All inputs are finite; a program needn't handle non-finite values.
Results may differ from a plain program's by a relative error of at most 0.0015.
Values may be sent and summed in bfloat16 or wider, within the bound.
A program may use at most 64 MiB of HBM per device.

v0:
```python
import math

import jax
import jax.numpy as jnp
from jax import lax
from jax.sharding import PartitionSpec as P

prior_mass = 1.0


def merged(value, axis, join):
    pieces = jax.tree.map(lambda part: lax.all_gather(part, axis), value)
    head = jax.tree.map(lambda part: part[0], pieces)
    tail = jax.tree.map(lambda part: part[1:], pieces)
    running, _ = lax.scan(lambda running, share: (join(running, share), None), head, tail)
    return running


def score_rows(row_block, centroids, half_sq, log_weight, scale_root):
    dots = lax.dot_general(
        row_block, centroids, (((1,), (1,)), ((), ())), preferred_element_type=jnp.float32
    )
    return (dots - half_sq[None, :]) / scale_root + log_weight[None, :]


def local(embeddings, centroids, log_weight):
    row_count, feat_dim = embeddings.shape
    local_count = centroids.shape[0]
    centre_vals = centroids.astype(jnp.float32)
    half_sq = 0.5 * jnp.sum(centre_vals * centre_vals, axis=1)
    scale_root = math.sqrt(feat_dim)
    groups = lax.axis_size("blk")
    gathered_count = row_count * groups
    block_len = math.gcd(gathered_count, 1024)

    def block_terms(row_block, log_part):
        logits = score_rows(row_block, centroids, half_sq, log_weight, scale_root)
        resp_vals = jnp.exp(logits - log_part[:, None])
        contrib = lax.dot_general(
            resp_vals.astype(jnp.bfloat16),
            row_block,
            (((0,), (0,)), ((), ())),
            preferred_element_type=jnp.float32,
        )
        return (contrib, jnp.sum(resp_vals, axis=0))

    shard_rows = lax.all_gather(embeddings, "blk", axis=0, tiled=True)
    logits = score_rows(shard_rows, centroids, half_sq, log_weight, scale_root)
    peak_val = jnp.max(logits, axis=1)
    peak_part = peak_val
    mass_part = jnp.sum(jnp.exp(logits - peak_val[:, None]), axis=1)
    peak_val = peak_part
    mass_sum = mass_part

    def combine(first_pair, later_pair):
        joined = jnp.maximum(first_pair[0], later_pair[0])
        return (
            joined,
            first_pair[1] * jnp.exp(first_pair[0] - joined)
            + later_pair[1] * jnp.exp(later_pair[0] - joined),
        )

    peak_val, mass_sum = merged((peak_val, mass_sum), "blk", combine)
    log_total = peak_val + jnp.log(mass_sum)
    empty_sums = jnp.zeros((local_count, feat_dim), jnp.float32)
    empty_counts = jnp.zeros((local_count,), jnp.float32)

    def advance(running, inputs):
        contrib, count_part = block_terms(inputs[0], inputs[1])
        return ((running[0] + contrib, running[1] + count_part), None)

    row_blocks = shard_rows.reshape(gathered_count // block_len, block_len, feat_dim)
    log_blocks = log_total.reshape(gathered_count // block_len, block_len)
    (weighted, counts), unused = lax.scan(
        advance, (empty_sums, empty_counts), (row_blocks, log_blocks)
    )
    weighted, counts = (
        lax.psum_scatter(weighted, "own", scatter_dimension=0, tiled=True),
        lax.psum_scatter(counts, "own", scatter_dimension=0, tiled=True),
    )
    owned_count = local_count // lax.axis_size("own")
    own_index = lax.axis_index("own")
    own_centres = lax.dynamic_slice_in_dim(centre_vals, own_index * owned_count, owned_count, 0)
    updated = (weighted + prior_mass * own_centres) / (counts[:, None] + prior_mass)
    log_norm = lax.dynamic_slice_in_dim(log_total, lax.axis_index("blk") * row_count, row_count, 0)
    return (updated, counts, log_norm)


def solution(mesh):
    placed = (P(("blk", "own"), None), P("blk", None), P("blk"))
    return jax.shard_map(
        local,
        mesh=mesh,
        in_specs=placed,
        out_specs=(P(("blk", "own"), None), P(("blk", "own")), P(("blk", "own"))),
        check_vma=False,
    )
```

profile of v0, /device:TPU:0, one launch (start us, length us, event | category | flops | bytes accessed | tf_op | source)
XLA Modules:
  0.0 181.1 jit_solution(10922595857111524906)
XLA Ops:
  7.2 0.0 all-gather.4.cloned.1.call-start
  7.2 0.7 all-gather.4.cloned.1.call-update
  7.9 0.0 reduce-scatter.2.cloned.1.call-start
  8.0 1.8 multiply_reduce_fusion
  9.8 0.0 copy-start.1
  9.8 48.7 %all-gather.4.cloned.1.call-done = bf16[2048,768]{1,0:T(8,128)(2,1)} async-done(((bf16[128,768]{1,0:T(8,128)(2,1)}), bf16[2048,768]{1,0:T(8,128)(2,1)}) %all-gather.4.cloned.1.call-update) | async-done | bytes 3145744 | tf_op jit(solution)/shard_map/all_gather | solution.py:47
  58.5 5.9 %fusion.20 = (f32[2048]{0:T(1024)S(1)}, f32[2048,1024]{0,1:T(8,128)S(1)}) fusion(f32[1024]{0:T(1024)} %param.9, f32[1024]{0:T(1024)S(1)} %broadcast_multiply_fusion, bf16[2048,768]{1,0:T(8,128)(2,1)} %all-gather.4.cloned.1.call-done, bf16[1024,768]{1,0:T(8,128)(2,1)} %param.8), kind=kOutput, calls=%fused_computation.24 | convolution fusion | flops 3229612032 | bytes 13123584 | tf_op jit(solution)/shard_map/dot_general | solution.py:20
  64.3 0.0 copy-done.1
  64.3 0.0 copy-start
  64.4 2.2 %exponential_reduce_fusion = f32[2048]{0:T(1024)S(1)} fusion(f32[2048,1024]{0,1:T(8,128)S(1)} %get-tuple-element.140, f32[2048]{0:T(1024)S(1)} %get-tuple-element.139, f32[1024]{0:T(1024)S(1)} %copy-done.1, f32[1024]{0:T(1024)S(1)} %broadcast_multiply_fusion), kind=kLoop, calls=%fused_computation.22 | loop fusion | flops 10483712 | bytes 8413184 | tf_op jit(solution)/shard_map/reduce_sum | solution.py:51
  66.6 19.1 %all-gather.1 = f32[32768]{0:T(1024)S(1)} all-gather(f32[2048]{0:T(1024)S(1)} %exponential_reduce_fusion), channel_id=3, replica_groups=mesh['blk'=16,'own'=2] {'blk'}, dimensions={0}, use_global_device_ids=true | all-gather | bytes 139264 | tf_op jit(solution)/shard_map/all_gather | solution.py:12
  85.7 17.8 %all-gather = f32[32768]{0:T(1024)S(1)} all-gather(f32[2048]{0:T(1024)S(1)} %get-tuple-element.139), channel_id=2, replica_groups=mesh['blk'=16,'own'=2] {'blk'}, dimensions={0}, use_global_device_ids=true | all-gather | bytes 139264 | tf_op jit(solution)/shard_map/all_gather | solution.py:12
  103.6 0.9 while.25
  104.6 0.0 copy-done
  104.6 24.8 %while.26 = (s32[]{:T(128)}, f32[1024,768]{1,0:T(8,128)}, f32[1024]{0:T(1024)S(1)}, bf16[2,1024,768]{2,1,0:T(8,128)(2,1)}, bf16[1024,768]{1,0:T(8,128)(2,1)S(1)}...) while((s32[]{:T(128)}, f32[1024,768]{1,0:T(8,128)}, ...), condition=%wide.region_7.8_spmd.clone, body=%wide.region_5.7_spmd.clone.sunk | while | flops 3233285120 | bytes 19448948 | solution.py:74
  104.6 5.4 %fusion.31 = (f32[1024]{0:T(1024)S(1)}, f32[1024,1024]{1,0:T(8,128)}) fusion(f32[1024]{0:T(1024)S(1)} %bitcast.31, f32[1024]{0:T(1024)S(1)} %get-tuple-element.277, f32[1024]{0:T(1024)S(1)} %get-tuple-element.276, bf16[1024,768]{1,0:T(8,128)(2,1)S(1)} %get-tuple-element.275, bf16[2,1024,768]{2,1,0:T(8,128)(2,1)} %get-tuple-element.274, ...), kind=kOutput, calls=%fused_computation.5.clone.1 | convolution fusion | flops 1615854592 | bytes 7356928 | tf_op jit(solution)/shard_map/while/body/eval_jaxpr/dot_general | solution.py:20
  110.0 6.5 %select_add_fusion.4 = f32[1024,768]{1,0:T(8,128)} fusion(f32[1024,768]{1,0:T(8,128)} %get-tuple-element.262, pred[]{:T(512)S(6)} %compare.3, f32[1024,1024]{1,0:T(8,128)} %get-tuple-element.231, f32[1024]{0:T(1024)S(1)} %bitcast.32, f32[1024]{0:T(1024)S(1)} %get-tuple-element.277, f32[1024]{0:T(1024)S(1)} %get-tuple-element.276, ...), kind=kOutput, calls=%fused_computation.4.clone.1 | convolution fusion | flops 1617428480 | bytes 12071425 | tf_op jit(solution)/shard_map/while/body/eval_jaxpr/dot_general | solution.py:39
  116.5 5.4 %fusion.31 = (f32[1024]{0:T(1024)S(1)}, f32[1024,1024]{1,0:T(8,128)}) fusion(f32[1024]{0:T(1024)S(1)} %bitcast.31, f32[1024]{0:T(1024)S(1)} %get-tuple-element.277, f32[1024]{0:T(1024)S(1)} %get-tuple-element.276, bf16[1024,768]{1,0:T(8,128)(2,1)S(1)} %get-tuple-element.275, bf16[2,1024,768]{2,1,0:T(8,128)(2,1)} %get-tuple-element.274, ...), kind=kOutput, calls=%fused_computation.5.clone.1 | convolution fusion | flops 1615854592 | bytes 7356928 | tf_op jit(solution)/shard_map/while/body/eval_jaxpr/dot_general | solution.py:20
  121.9 7.5 %select_add_fusion.4 = f32[1024,768]{1,0:T(8,128)} fusion(f32[1024,768]{1,0:T(8,128)} %get-tuple-element.262, pred[]{:T(512)S(6)} %compare.3, f32[1024,1024]{1,0:T(8,128)} %get-tuple-element.231, f32[1024]{0:T(1024)S(1)} %bitcast.32, f32[1024]{0:T(1024)S(1)} %get-tuple-element.277, f32[1024]{0:T(1024)S(1)} %get-tuple-element.276, ...), kind=kOutput, calls=%fused_computation.4.clone.1 | convolution fusion | flops 1617428480 | bytes 12071425 | tf_op jit(solution)/shard_map/while/body/eval_jaxpr/dot_general | solution.py:39
  129.4 0.0 reduce-scatter.2.cloned.1.call-update
  129.4 0.0 copy-start.2
  129.5 1.6 convert_element_type.6
  131.1 0.0 copy-done.2
  131.1 0.6 dynamic-slice
  132.4 0.6 dynamic_slice.22
  133.0 5.1 %all-reduce = f32[1024]{0:T(1024)S(1)} all-reduce(f32[1024]{0:T(1024)S(1)} %get-tuple-element.77), channel_id=5, replica_groups=mesh['blk'=16,'own'=2] {'own'}, use_global_device_ids=true, to_apply=%region_9.10.clone | all-reduce | flops 1024 | bytes 8192
  138.1 0.7 broadcast_add_fusion
  138.7 32.7 %reduce-scatter.2.cloned.1.call-done = f32[512,768]{1,0:T(8,128)} async-done(((f32[1024,768]{1,0:T(8,128)}), f32[512,768]{1,0:T(8,128)}) %reduce-scatter.2.cloned.1.call-update) | async-done | bytes 1572880 | tf_op jit(solution)/shard_map/reduce_scatter | solution.py:78
  171.5 2.8 %add_divide_fusion = f32[512,768]{1,0:T(8,128)} fusion(f32[512,768]{1,0:T(8,128)} %reduce-scatter.2.cloned.1.call-done, f32[1024,768]{1,0:T(8,128)S(1)} %convert_element_type.6, s32[]{:T(128)S(6)} %select_n.6, f32[512]{0:T(512)S(1)} %get-tuple-element.133), kind=kLoop, calls=%fused_computation.26 | loop fusion | flops 786432 | bytes 4720644 | tf_op jit(solution)/shard_map/div | solution.py:84
  (45 shorter events, 0.6 us)
Async XLA Ops:
  7.2 51.3 %all-gather.4.cloned.1.call-start = ((), (), s32[]{:S(2)}) async-start(), calls=%async_computation.1 | async-start | bytes 3342336 | tf_op jit(solution)/shard_map/all_gather | solution.py:47
  7.9 163.6 %reduce-scatter.2.cloned.1.call-start = ((), (), s32[]{:S(2)}) async-start(), calls=%async_computation.2 | async-start | bytes 4718592 | tf_op jit(solution)/shard_map/reduce_scatter | solution.py:78
  9.8 54.6 %copy-start.1 = (f32[1024]{0:T(1024)S(1)}, f32[1024]{0:T(1024)}, u32[]{:S(2)}) copy-start(f32[1024]{0:T(1024)} %param.9) | copy-start | bytes 12292
  64.3 40.2 %copy-start = (bf16[1024,768]{1,0:T(8,128)(2,1)S(1)}, bf16[1024,768]{1,0:T(8,128)(2,1)}, u32[]{:S(2)}) copy-start(bf16[1024,768]{1,0:T(8,128)(2,1)} %param.8) | copy-start | bytes 4718596
  129.4 1.7 copy-start.2
Sparse Core Ops, SparseCore 0:
  10.3 48.1 all-gather.3
  129.6 41.8 reduce-scatter.1
where the time goes:
time: 181 us
  waiting for transfers between devices  82.1 us (45%)
  blocking collectives  42 us (23%)
  matrix products  30.6 us (17%)
  between operations  14.9 us (8%)
  other arithmetic  9.31 us (5%)
    all_gather x1, waiting for transfers between devices, local(): shard_rows = lax.all_gather(embeddings, 'blk', axis=0, tiled=True)  48.7 us
    all_gather x2, blocking collectives, merged(): pieces = jax.tree.map(lambda part: lax.all_gather(part, axis), value)  36.9 us
    reduce_scatter x1, waiting for transfers between devices, local(): lax.psum_scatter(weighted, 'own', scatter_dimension=0, tiled=True)  32.7 us
    dot_general x3, matrix products, score_rows(): lax.dot_general(row_block, centroids, (((1,), (1,)), ((), ())), preferred...  16.6 us
    dot_general x2, matrix products, block_terms(): lax.dot_general(resp_vals.astype(jnp.bfloat16), row_block, (((0,), (0,)),...  14 us
    unnamed x1, blocking collectives  5.12 us
  transfers between devices with their start and end apart: 2, of which 2 were waited for; matrix products, arithmetic and copies ran while one was open for 3% of the time, Pallas kernels for 0%

commit v1 on v0

--- a/solution.py
+++ b/solution.py
@@ -1,11 +1,17 @@
+import functools
 import math
 
 import jax
 import jax.numpy as jnp
 from jax import lax
+from jax.experimental import pallas as pl
+from jax.experimental.pallas import tpu as pltpu
 from jax.sharding import PartitionSpec as P
 
 prior_mass = 1.0
+MESH = pl.DeviceIdType.MESH
+PIECES = 4
+LANES = 128
 
 
 def merged(value, axis, join):
@@ -86,10 +92,352 @@
     return (updated, counts, log_norm)
 
 
+def row_to_column(row):
+    eye = lax.broadcasted_iota(jnp.int32, (LANES, LANES), 0) == lax.broadcasted_iota(
+        jnp.int32, (LANES, LANES), 1
+    )
+    return jnp.sum(jnp.where(eye, jnp.broadcast_to(row, (LANES, LANES)), 0.0), axis=1, keepdims=True)
+
+
+def column_to_row(column):
+    eye = lax.broadcasted_iota(jnp.int32, (LANES, LANES), 0) == lax.broadcasted_iota(
+        jnp.int32, (LANES, LANES), 1
+    )
+    return jnp.sum(
+        jnp.where(eye, jnp.broadcast_to(column, (LANES, LANES)), 0.0), axis=0, keepdims=True
+    )
+
+
+def join_logs(parts):
+    top = functools.reduce(jnp.maximum, parts)
+    return top + jnp.log2(sum(jnp.exp2(part - top) for part in parts))
+
+
+def kernel(
+    depth,
+    x_ref,
+    c_hbm,
+    lw_ref,
+    new_ref,
+    counts_ref,
+    log_ref,
+    xall,
+    cen,
+    bias,
+    expd,
+    peaks,
+    resp,
+    total,
+    mass,
+    stat1,
+    got1,
+    stat2,
+    got2,
+    sem_in,
+    send_z,
+    recv_z,
+    send_x,
+    recv_x,
+    send_y,
+    recv_y,
+    send_dx,
+    recv_dx,
+    send_dy,
+    recv_dy,
+    send_c,
+    recv_c,
+    send_s1,
+    recv_s1,
+    send_s2,
+    recv_s2,
+):
+    blk, own = lax.axis_index("blk"), lax.axis_index("own")
+    core = blk % 2
+    px = (blk // 2) % 2
+    qz = blk // 4
+    local_count, feat = cen.shape
+    per = x_ref.shape[0] // PIECES
+    half = per // 2
+    piece_rows = xall.shape[1]
+    sub = piece_rows // depth
+    tiles = sub // LANES
+    log2e = math.log2(math.e)
+
+    def device(q, p, o, c):
+        return ((q * 2 + p) * 2 + c, o)
+
+    def slot(q, p, o, c):
+        return ((q * 2 + p) * 2 + o) * 2 + c
+
+    def rows_of(j, q, p, o, c, start=0, count=None):
+        first = pl.multiple_of(slot(q, p, o, c) * per + start, half)
+        return xall.at[j, pl.ds(first, per if count is None else count), :]
+
+    def zback(d):
+        return (qz + depth - d) % depth
+
+    x_dev = device(qz, 1 - px, own, core)
+    y_dev = device(qz, px, 1 - own, core)
+    c_dev = device(qz, px, own, 1 - core)
+    z_devs = [None] + [device((qz + d) % depth, px, own, core) for d in range(1, depth)]
+    plane = [None]
+    for mask in range(1, 8):
+        p = 1 - px if mask & 1 else px
+        o = 1 - own if mask & 2 else own
+        c = 1 - core if mask & 4 else core
+        plane.append(device(qz, p, o, c))
+    started = []
+
+    def push(src, dst, send, recv, dev):
+        copy = pltpu.make_async_remote_copy(
+            src_ref=src, dst_ref=dst, send_sem=send, recv_sem=recv, device_id=dev, device_id_type=MESH
+        )
+        copy.start()
+        started.append(copy)
+
+    def arrive(dst, recv):
+        pltpu.make_async_remote_copy(
+            src_ref=dst, dst_ref=dst, send_sem=recv, recv_sem=recv, device_id=x_dev, device_id_type=MESH
+        ).wait_recv()
+
+    first_row = pl.multiple_of(own * local_count, local_count)
+    cen_copy = pltpu.make_async_copy(c_hbm.at[pl.ds(first_row, local_count), :], cen, sem_in.at[0])
+    cen_copy.start()
+    own_copies = []
+    for j in range(PIECES):
+        copy = pltpu.make_async_copy(
+            x_ref.at[pl.ds(j * per, per), :], rows_of(j, qz, px, own, core), sem_in.at[1 + j]
+        )
+        copy.start()
+        own_copies.append(copy)
+
+    barrier = pltpu.get_barrier_semaphore()
+    partners = z_devs[1:] + plane[1:]
+    for dev in partners:
+        pl.semaphore_signal(barrier, inc=1, device_id=dev, device_id_type=MESH)
+    pl.semaphore_wait(barrier, len(partners))
+
+    def send_own(j):
+        src = x_ref.at[pl.ds(j * per, per), :]
+        dst = rows_of(j, qz, px, own, core)
+        push(src, dst, send_x.at[j, 0], recv_x.at[j, 0], x_dev)
+        push(src, dst, send_y.at[j, 0], recv_y.at[j, 0], y_dev)
+        for d in range(1, depth):
+            push(src, dst, send_z.at[j, d], recv_z.at[j, d], z_devs[d])
+        push(src, dst, send_c.at[j, 0, 0], recv_c.at[j, 0, 0], c_dev)
+
+    def on_z(j, d):
+        block = rows_of(j, zback(d), px, own, core)
+        arrive(block, recv_z.at[j, d])
+        push(block, block, send_x.at[j, d], recv_x.at[j, d], x_dev)
+        push(block, block, send_y.at[j, d], recv_y.at[j, d], y_dev)
+        push(block, block, send_c.at[j, 0, d], recv_c.at[j, 0, d], c_dev)
+
+    def on_xy(j, d):
+        q = zback(d)
+        block = rows_of(j, q, 1 - px, own, core)
+        arrive(block, recv_x.at[j, d])
+        part = rows_of(j, q, 1 - px, own, core, 0, half)
+        push(part, part, send_dy.at[j, d], recv_dy.at[j, d], y_dev)
+        push(block, block, send_c.at[j, 1, d], recv_c.at[j, 1, d], c_dev)
+        block = rows_of(j, q, px, 1 - own, core)
+        arrive(block, recv_y.at[j, d])
+        part = rows_of(j, q, px, 1 - own, core, half, half)
+        push(part, part, send_dx.at[j, d], recv_dx.at[j, d], x_dev)
+        push(block, block, send_c.at[j, 2, d], recv_c.at[j, 2, d], c_dev)
+
+    def on_diag(j, d):
+        q = zback(d)
+        arrive(rows_of(j, q, 1 - px, 1 - own, core, 0, half), recv_dy.at[j, d])
+        arrive(rows_of(j, q, 1 - px, 1 - own, core, half, half), recv_dx.at[j, d])
+        block = rows_of(j, q, 1 - px, 1 - own, core)
+        push(block, block, send_c.at[j, 3, d], recv_c.at[j, 3, d], c_dev)
+
+    def on_core(j):
+        own_copies[j].wait()
+        for d in range(depth):
+            q = zback(d)
+            for kind, (p, o) in enumerate(
+                ((px, own), (1 - px, own), (px, 1 - own), (1 - px, 1 - own))
+            ):
+                arrive(rows_of(j, q, p, o, 1 - core), recv_c.at[j, kind, d])
+
+    def arrivals(j):
+        groups = []
+        for t in range(depth):
+            def group(t=t):
+                if t == 0 and j + 1 < PIECES:
+                    send_own(j + 1)
+                if t == 0 and depth > 1:
+                    on_z(j, 1)
+                if t + 2 < depth:
+                    on_z(j, t + 2)
+                on_xy(j, t)
+                if t >= 1:
+                    on_diag(j, t - 1)
+                if t == depth - 1:
+                    on_diag(j, t)
+                    on_core(j)
+            groups.append(group)
+        return groups
+
+    def first_pass(j, t):
+        rows = xall[j, pl.ds(t * sub, sub), :]
+        dots = lax.dot_general(
+            cen[...], rows, (((1,), (1,)), ((), ())), preferred_element_type=jnp.float32
+        )
+        logits = dots * (log2e / math.sqrt(feat)) + bias[...]
+        peak = jnp.max(logits, axis=0, keepdims=True)
+        vals = jnp.exp2(logits - peak)
+        expd[j, t] = vals
+        peaks[j, t] = peak
+        logs = peak + jnp.log2(jnp.sum(vals, axis=0, keepdims=True))
+        for i in range(tiles):
+            stat1[j, pl.ds(t * tiles + i, 1), :] = logs[:, i * LANES : (i + 1) * LANES]
+
+    def stats_send(j):
+        for mask in range(1, 8):
+            push(
+                stat1.at[j], got1.at[j, mask], send_s1.at[j, mask], recv_s1.at[j, mask], plane[mask]
+            )
+
+    def stats_mid(j):
+        for mask in range(1, 8):
+            arrive(got1.at[j, mask], recv_s1.at[j, mask])
+        stat2[j] = join_logs([stat1[j]] + [got1[j, mask] for mask in range(1, 8)])
+        for d in range(1, depth):
+            push(stat2.at[j], got2.at[j, d], send_s2.at[j, d], recv_s2.at[j, d], z_devs[d])
+
+    def stats_end(j):
+        for d in range(1, depth):
+            arrive(got2.at[j, d], recv_s2.at[j, d])
+        log_ref[j] = join_logs([stat2[j]] + [got2[j, d] for d in range(1, depth)])
+
+    def second_pass(j, part, parts):
+        width = depth // parts
+        for t in range(part * width, (part + 1) * width):
+            norm = jnp.concatenate(
+                [log_ref[j, pl.ds(t * tiles + i, 1), :] for i in range(tiles)], axis=1
+            )
+            vals = expd[j, t] * jnp.exp2(peaks[j, t] - norm)
+            mass[...] += sum(vals[:, i * LANES : (i + 1) * LANES] for i in range(tiles))
+            k = t - part * width
+            resp[:, k * sub : (k + 1) * sub] = vals.astype(jnp.bfloat16)
+        span = width * sub
+        total[...] += jnp.dot(
+            resp[:, :span],
+            xall[j, pl.ds(part * span, span), :],
+            preferred_element_type=jnp.float32,
+        )
+
+    send_own(0)
+    cen_copy.wait()
+    total[...] = jnp.zeros_like(total)
+    mass[...] = jnp.zeros_like(mass)
+    for i in range(local_count // LANES):
+        span = pl.ds(i * LANES, LANES)
+        vals = cen[span, :].astype(jnp.float32)
+        half_sq = 0.5 * jnp.sum(vals * vals, axis=1, keepdims=True)
+        weight = row_to_column(lw_ref[pl.ds(own * (local_count // LANES) + i, 1), :])
+        column = (weight - half_sq / math.sqrt(feat)) * log2e
+        bias[span, :] = jnp.broadcast_to(column, (LANES, sub))
+    for group in arrivals(0):
+        group()
+    for j in range(PIECES):
+        groups = arrivals(j + 1) if j + 1 < PIECES else []
+        for t in range(depth):
+            if groups:
+                groups[t]()
+            first_pass(j, t)
+            if j >= 1 and t == depth // 2 - 1:
+                stats_mid(j - 1)
+            if j >= 1 and t == depth - 1:
+                stats_end(j - 1)
+            if j >= 2 and t % 2 == 0:
+                second_pass(j - 2, t // 2, depth // 2)
+        stats_send(j)
+    last = PIECES - 1
+    second_pass(last - 1, 0, 2)
+    stats_mid(last)
+    second_pass(last - 1, 1, 2)
+    stats_end(last)
+    second_pass(last, 0, 2)
+    second_pass(last, 1, 2)
+    for i in range(local_count // LANES):
+        span = pl.ds(i * LANES, LANES)
+        counts = jnp.sum(mass[span, :], axis=1, keepdims=True)
+        counts_ref[pl.ds(i, 1), :] = column_to_row(counts)
+        new_ref[span, :] = (total[span, :] + prior_mass * cen[span, :].astype(jnp.float32)) / (
+            counts + prior_mass
+        )
+    for copy in started:
+        copy.wait_send()
+
+
+def fused(blk_size, own_size, embeddings, centroids, log_weight):
+    row_count, feat = embeddings.shape
+    local_count = centroids.shape[0] // own_size
+    depth = blk_size // 4
+    piece_rows = row_count * blk_size * own_size // PIECES
+    vmem = PIECES * piece_rows * (feat * 2 + local_count * 4)
+    fits = (
+        own_size == 2
+        and blk_size % 16 == 0
+        and row_count % (32 * PIECES) == 0
+        and local_count % LANES == 0
+        and centroids.shape[0] % LANES == 0
+        and vmem < 40 * 2**20
+    )
+    if not fits:
+        return local(embeddings, centroids, log_weight)
+    sub = piece_rows // depth
+    tile = (PIECES, piece_rows // LANES, LANES)
+    dma = pltpu.SemaphoreType.DMA
+    vm = pl.BlockSpec(memory_space=pltpu.VMEM)
+    updated, counts, logs = pl.pallas_call(
+        functools.partial(kernel, depth),
+        out_shape=(
+            jax.ShapeDtypeStruct((local_count, feat), jnp.float32),
+            jax.ShapeDtypeStruct((local_count // LANES, LANES), jnp.float32),
+            jax.ShapeDtypeStruct(tile, jnp.float32),
+        ),
+        in_specs=[vm, pl.BlockSpec(memory_space=pl.ANY), vm],
+        out_specs=(vm, vm, vm),
+        scratch_shapes=[
+            pltpu.VMEM((PIECES, piece_rows, feat), jnp.bfloat16),
+            pltpu.VMEM((local_count, feat), jnp.bfloat16),
+            pltpu.VMEM((local_count, sub), jnp.float32),
+            pltpu.VMEM((PIECES, depth, local_count, sub), jnp.float32),
+            pltpu.VMEM((PIECES, depth, 1, sub), jnp.float32),
+            pltpu.VMEM((local_count, piece_rows // 2), jnp.bfloat16),
+            pltpu.VMEM((local_count, feat), jnp.float32),
+            pltpu.VMEM((local_count, LANES), jnp.float32),
+            pltpu.VMEM(tile, jnp.float32),
+            pltpu.VMEM((PIECES, 8) + tile[1:], jnp.float32),
+            pltpu.VMEM(tile, jnp.float32),
+            pltpu.VMEM((PIECES, depth) + tile[1:], jnp.float32),
+            dma((1 + PIECES,)),
+        ]
+        + [dma((PIECES, depth))] * 10
+        + [dma((PIECES, 4, depth))] * 2
+        + [dma((PIECES, 8))] * 2
+        + [dma((PIECES, depth))] * 2,
+        compiler_params=pltpu.CompilerParams(
+            collective_id=0, has_side_effects=True, vmem_limit_bytes=56 * 2**20
+        ),
+    )(embeddings, centroids, log_weight.reshape(-1, LANES))
+    place = lax.axis_index("blk")
+    spot = ((place // 2) * own_size + lax.axis_index("own")) * 2 + place % 2
+    mine = lax.dynamic_slice_in_dim(
+        logs.reshape(PIECES, blk_size * own_size, row_count // PIECES), spot, 1, 1
+    )
+    return (updated, counts.reshape(-1), mine.reshape(-1) * math.log(2.0))
+
+
 def solution(mesh):
     placed = (P(("blk", "own"), None), P("blk", None), P("blk"))
     return jax.shard_map(
-        local,
+        functools.partial(fused, mesh.shape["blk"], mesh.shape["own"]),
         mesh=mesh,
         in_specs=placed,
         out_specs=(P(("blk", "own"), None), P(("blk", "own")), P(("blk", "own"))),

time: 181 us -> 82.7 us (0.46)
  waiting for transfers between devices: 82.1 us -> 0 us
  Pallas kernels: 0 us -> 77.1 us
  blocking collectives: 42 us -> 0 us
  matrix products: 30.6 us -> 0 us
  between operations: 14.9 us -> 0.68 us
  other arithmetic: 9.31 us -> 0.01 us
  local copies, waits for them, and re-layouts: 1.58 us -> 4.63 us
    pallas_call x0 -> x1, Pallas kernels: none -> 77.1 us  [fused(): pl.pallas_call(functools.partial(kernel, depth), out_shape=(jax.ShapeDtyp...]
    all_gather x1 -> x0, waiting for transfers between devices: 48.7 us -> none  [local(): shard_rows = lax.all_gather(embeddings, 'blk', axis=0, tiled=True)]
    all_gather x2 -> x0, blocking collectives: 36.9 us -> none  [merged(): pieces = jax.tree.map(lambda part: lax.all_gather(part, axis), value)]
    reduce_scatter x1 -> x0, waiting for transfers between devices: 32.7 us -> none  [local(): lax.psum_scatter(weighted, 'own', scatter_dimension=0, tiled=True)]
    dot_general x5 -> x0, matrix products: 30.6 us -> none  [the longest x3 16.6 us: score_rows(): lax.dot_general(row_block, centroids, (((1,), (1,)), ((), ())), preferred...]
    unnamed x1 -> x0, blocking collectives: 5.12 us -> none
    reduce_sum x2 -> x0, other arithmetic: 4.02 us -> none  [the longest x1 2.23 us: local(): mass_part = jnp.sum(jnp.exp(logits - peak_val[:, None]), axis=1)]
    div x1 -> x0, other arithmetic: 2.78 us -> none  [local(): (weighted + prior_mass * own_centres) / (counts[:, None] + prior_mass)]
  transfers between devices with their start and end apart: 2 -> 0, of which waited for: 2 -> 0; matrix products, arithmetic and copies ran while one was open for 3% -> 0% of each run, Pallas kernels for 0% -> 0%
where the time goes in v1:
time: 82.7 us; the launch traced here: 82.4 us
  Pallas kernels  77.1 us (93%)
  local copies, waits for them, and re-layouts  4.63 us (6%)
    pallas_call x1, Pallas kernels, fused(): pl.pallas_call(functools.partial(kernel, depth), out_shape=(jax.ShapeDtyp...  77.1 us
    unnamed x4, local copies, waits for them, and re-layouts  3.23 us

profile of v1, /device:TPU:0, one launch (start us, length us, event | category | flops | bytes accessed | tf_op | source)
XLA Modules:
  0.0 82.4 jit_solution(13620273006469716304)
XLA Ops:
  0.7 77.1 %shard_map.58 = (f32[512,768]{1,0:T(8,128)}, f32[4,128]{1,0:T(4,128)}, f32[4,8,128]{2,1,0:T(8,128)}) custom-call(bf16[128,768]{1,0:T(8,128)(2,1)} %x_ref.1, bf16[1024,768]{1,0:T(8,128)(2,1)} %c_hbm.1, f32[8,128]{1,0:T(8,128)} %bitcast.6), custom_call_target="tpu_custom_call" | custom-call | tf_op jit(solution)/shard_map/pallas_call | solution.py:397
  77.7 0.8 reshape.20
  78.6 0.6 mul.19
  79.1 0.0 copy-start
  79.1 2.7 %copy.10 = f32[512,768]{1,0:T(8,128)} copy(f32[512,768]{1,0:T(8,128)} %get-tuple-element.12) | data formatting | bytes 3145728
  81.8 0.0 copy-done
  81.8 0.6 copy.11
  (2 shorter events, 0.0 us)
Async XLA Ops:
  79.1 2.7 %copy-start = (f32[4,128]{1,0:T(4,128)S(1)}, f32[4,128]{1,0:T(4,128)}, u32[]{:S(2)}) copy-start(f32[4,128]{1,0:T(4,128)} %get-tuple-element.7) | copy-start | bytes 6148

commit v2 on v1

--- a/solution.py
+++ b/solution.py
@@ -11,6 +11,7 @@
 prior_mass = 1.0
 MESH = pl.DeviceIdType.MESH
 PIECES = 4
+AHEAD = 2
 LANES = 128
 
 
@@ -262,24 +263,19 @@
             ):
                 arrive(rows_of(j, q, p, o, 1 - core), recv_c.at[j, kind, d])
 
-    def arrivals(j):
-        groups = []
-        for t in range(depth):
-            def group(t=t):
-                if t == 0 and j + 1 < PIECES:
-                    send_own(j + 1)
-                if t == 0 and depth > 1:
-                    on_z(j, 1)
-                if t + 2 < depth:
-                    on_z(j, t + 2)
-                on_xy(j, t)
-                if t >= 1:
-                    on_diag(j, t - 1)
-                if t == depth - 1:
-                    on_diag(j, t)
-                    on_core(j)
-            groups.append(group)
-        return groups
+    def stage(k):
+        steps = []
+        if k < PIECES:
+            steps += [lambda: on_xy(k, 0)]
+            steps += [functools.partial(on_z, k, d) for d in range(1, depth)]
+        if 0 <= k - 2 < PIECES:
+            steps += [functools.partial(on_diag, k - 2, d) for d in range(depth)]
+        if 0 <= k - 1 < PIECES:
+            steps += [functools.partial(on_xy, k - 1, d) for d in range(1, depth)]
+        if 0 <= k - 2 < PIECES:
+            steps += [lambda: on_core(k - 2)]
+        size = -(-len(steps) // depth)
+        return [steps[t * size : (t + 1) * size] for t in range(depth)]
 
     def first_pass(j, t):
         rows = xall[j, pl.ds(t * sub, sub), :]
@@ -330,7 +326,8 @@
             preferred_element_type=jnp.float32,
         )
 
-    send_own(0)
+    for j in range(min(AHEAD, PIECES)):
+        send_own(j)
     cen_copy.wait()
     total[...] = jnp.zeros_like(total)
     mass[...] = jnp.zeros_like(mass)
@@ -341,22 +338,27 @@
         weight = row_to_column(lw_ref[pl.ds(own * (local_count // LANES) + i, 1), :])
         column = (weight - half_sq / math.sqrt(feat)) * log2e
         bias[span, :] = jnp.broadcast_to(column, (LANES, sub))
-    for group in arrivals(0):
-        group()
-    for j in range(PIECES):
-        groups = arrivals(j + 1) if j + 1 < PIECES else []
+    lag = 3
+    for k in range(PIECES + lag):
+        if AHEAD <= k + AHEAD < PIECES:
+            send_own(k + AHEAD)
+        groups = stage(k)
+        j = k - lag
         for t in range(depth):
-            if groups:
-                groups[t]()
-            first_pass(j, t)
-            if j >= 1 and t == depth // 2 - 1:
+            for step in groups[t]:
+                step()
+            if 0 <= j:
+                first_pass(j, t)
+            if j >= 1 and t == depth - 1:
                 stats_mid(j - 1)
-            if j >= 1 and t == depth - 1:
-                stats_end(j - 1)
+            if j >= 2 and t == 0:
+                stats_end(j - 2)
             if j >= 2 and t % 2 == 0:
                 second_pass(j - 2, t // 2, depth // 2)
-        stats_send(j)
+        if 0 <= j:
+            stats_send(j)
     last = PIECES - 1
+    stats_end(last - 1)
     second_pass(last - 1, 0, 2)
     stats_mid(last)
     second_pass(last - 1, 1, 2)

time: 82.7 us -> 69.4 us (0.84)
  Pallas kernels: 77.1 us -> 63.8 us
    pallas_call x1, Pallas kernels: 77.1 us -> 63.8 us  [fused(): pl.pallas_call(functools.partial(kernel, depth), out_shape=(jax.ShapeDtyp...]
where the time goes in v2:
time: 69.4 us; the launch traced here: 69.1 us
  Pallas kernels  63.8 us (92%)
  local copies, waits for them, and re-layouts  4.63 us (7%)
    pallas_call x1, Pallas kernels, fused(): pl.pallas_call(functools.partial(kernel, depth), out_shape=(jax.ShapeDtyp...  63.8 us
    unnamed x4, local copies, waits for them, and re-layouts  3.23 us

profile of v2, /device:TPU:0, one launch (start us, length us, event | category | flops | bytes accessed | tf_op | source)
XLA Modules:
  0.0 69.1 jit_solution(6839701382725511562)
XLA Ops:
  0.7 63.8 %shard_map.58 = (f32[512,768]{1,0:T(8,128)}, f32[4,128]{1,0:T(4,128)}, f32[4,8,128]{2,1,0:T(8,128)}) custom-call(bf16[128,768]{1,0:T(8,128)(2,1)} %x_ref.1, bf16[1024,768]{1,0:T(8,128)(2,1)} %c_hbm.1, f32[8,128]{1,0:T(8,128)} %bitcast.6), custom_call_target="tpu_custom_call" | custom-call | tf_op jit(solution)/shard_map/pallas_call | solution.py:399
  64.5 0.8 %reshape.20 = f32[4,32,32]{2,1,0:T(8,128)S(1)} reshape(f32[4,8,128]{2,1,0:T(8,128)} %get-tuple-element.8) | data formatting | bytes 32768 | tf_op jit(solution)/shard_map/reshape | solution.py:434
  65.3 0.6 mul.19
  65.9 0.0 copy-start
  65.9 2.7 %copy.10 = f32[512,768]{1,0:T(8,128)} copy(f32[512,768]{1,0:T(8,128)} %get-tuple-element.12) | data formatting | bytes 3145728
  68.5 0.0 copy-done
  68.5 0.6 copy.11
  (2 shorter events, 0.0 us)
Async XLA Ops:
  65.9 2.7 %copy-start = (f32[4,128]{1,0:T(4,128)S(1)}, f32[4,128]{1,0:T(4,128)}, u32[]{:S(2)}) copy-start(f32[4,128]{1,0:T(4,128)} %get-tuple-element.7) | copy-start | bytes 6148
